TPU v7x, 32 devices: a whole 2x2x4 slice. The times are simulated.
32 devices in a mesh: band: 16 (over z, y, x), ga: 2 (over core).
Axes of the slice: x: 2, y: 2, z: 4, core: 2. Of those that a mesh axis runs over, the one named last changes fastest.
Arguments:
- matrix_elements: float32 [2, 4096, 12288], P(None, 'band', 'ga'), may hold values from -6 to 6
- band_index: int32 [4096], P('band'), may hold values from 0 to 1048575
- occupied: int32 [1], replicated, may hold values from 262144 to 786432
- band_weight: float32 [4096], P('band'), may hold values from 0.3 to 3
- coulomb: float32 [12288], replicated, may hold values from 0.2 to 5
Outputs:
- sigma: float32 [12288, 2, 512], P(('ga', 'band'))
All inputs are finite; a program needn't handle non-finite values.
Results may differ from a plain program's by a relative error of at most 0.00018.
Values sent between devices are 32-bit elements; how exact they have to be, the bound alone decides.
A program may use at most 192 MiB of HBM per device.

v0:
```python
import math
import jax
import jax.numpy as jnp
from jax import lax
from jax.sharding import PartitionSpec as P

COLS = 512


def spread(x, axis, root):
    mine = lax.axis_index(axis) == root
    return lax.psum(jnp.where(mine, x, jnp.zeros_like(x)), axis)


def contract(left, right):
    return lax.dot_general(
        left,
        right,
        (((0,), (0,)), ((), ())),
        precision=lax.Precision.HIGHEST,
        preferred_element_type=jnp.float32,
    )


def right_side(slab):
    return jnp.concatenate(
        [jnp.concatenate([slab[0], slab[1]], 1), jnp.concatenate([slab[1], -slab[0]], 1)], 0
    )


def defects(coef, block):
    square = 2.0 - block[0] * block[0] - block[1] * block[1]
    return jnp.dot(
        coef, square, precision=lax.Precision.HIGHEST, preferred_element_type=jnp.float32
    )


def body(matrix_elements, band_index, occupied, band_weight, coulomb):
    bands_dev = matrix_elements.shape[1]
    half = matrix_elements.shape[2]
    n_band = lax.axis_size("band")
    rows_dev = half // n_band
    factor = 1.0 / math.sqrt(bands_dev * n_band)
    occ = (band_index < occupied[0]).astype(jnp.float32)
    coef = (0.5 - occ) * band_weight
    slab = spread(matrix_elements[:, :, :COLS], "ga", 0)
    band_pos = lax.axis_index("band")
    ga_pos = lax.axis_index("ga")
    left = jnp.concatenate(
        [coef[:, None] * matrix_elements[0], coef[:, None] * matrix_elements[1]], 0
    )
    right = right_side(slab)
    sums = lax.psum_scatter(contract(left, right), "band", scatter_dimension=0, tiled=True)
    defect_full = defects(coef, matrix_elements)
    defect_slab = defects(coef, slab)
    row_def = lax.psum_scatter(defect_full, "band", scatter_dimension=0, tiled=True)
    col_def = lax.psum(defect_slab, "band")
    sums = sums * factor
    row_def = row_def * factor
    col_def = col_def * factor
    row_coul = lax.dynamic_slice_in_dim(coulomb, ga_pos * half + band_pos * rows_dev, rows_dev, 0)
    weight = jnp.sqrt(row_coul[:, None] * coulomb[None, :COLS])
    part_re = weight * (sums[:, :COLS] + 0.5 * (row_def[:, None] + col_def[None, :]))
    part_im = weight * sums[:, COLS:]
    return jnp.stack([part_re, part_im], 1)


def solution(mesh):
    return jax.shard_map(
        body,
        mesh=mesh,
        in_specs=(P(None, "band", "ga"), P("band"), P(), P("band"), P()),
        out_specs=P(("ga", "band"), None, None),
        check_vma=False,
    )
```

profile of v0, /device:TPU:0, one launch (start us, length us, event | category | flops | bytes accessed | tf_op | source)
XLA Modules:
  0.0 451.3 jit_solution(16196607224541450727)
XLA Ops:
  6.5 2.3 slice_select_fusion
  8.8 0.0 all-reduce.4.cloned.1.call-update
  8.8 0.0 reduce-scatter.2.cloned.1.call-start
  9.5 0.7 fusion.29
  10.2 11.4 %bitcast_multiply_fusion.3 = (f32[256,6144]{1,0:T(8,128)}, f32[256,6144]{1,0:T(8,128)}) fusion(f32[2,256,6144]{2,1,0:T(8,128)} %param.5, f32[256]{0:T(256)S(1)} %fusion.29), kind=kLoop, calls=%fused_computation.9 | loop fusion | flops 3145728 | bytes 25166848 | tf_op jit(solution)/shard_map/mul | solution.py:50
  21.6 10.2 %all-reduce.4.cloned.1.call-done = f32[2,256,512]{2,1,0:T(8,128)} async-done(((f32[2,256,512]{2,1,0:T(8,128)}), f32[2,256,512]{2,1,0:T(8,128)}) %all-reduce.4.cloned.1.call-update) | async-done | bytes 1048592 | tf_op jit(solution)/shard_map/psum | solution.py:12
  31.8 1.1 fusion.33
  32.9 1.3 slice_bitcast_fusion.1
  34.2 44.8 %fusion = f32[6144,1024]{1,0:T(8,128)} fusion(f32[256,6144]{1,0:T(8,128)} %get-tuple-element.8, f32[256,6144]{1,0:T(8,128)} %get-tuple-element.7, f32[256,512]{1,0:T(8,128)S(1)} %fusion.33, f32[256,512]{1,0:T(8,128)S(1)} %get-tuple-element.12, f32[256,512]{1,0:T(8,128)S(1)} %get-tuple-element.11), kind=kOutput, calls=%fused_computation | convolution fusion | flops 38659424256 | bytes 39321600 | tf_op jit(solution)/shard_map/dot_general | solution.py:16
  79.0 0.0 reduce-scatter.2.cloned.1.call-update
  79.0 0.7 copy-done.1
  79.8 0.1 dynamic_slice.3
  79.8 0.0 copy-done.2
  79.8 0.6 dynamic-slice
  81.1 0.0 slice-start
  81.1 8.5 %fusion.5 = f32[1,6144]{1,0:T(1,128)S(1)} fusion(f32[256,1]{0,1:T(1,128)S(1)} %bitcast.40, f32[2,256,6144]{2,1,0:T(8,128)} %param.5), kind=kOutput, calls=%fused_computation.7 | convolution fusion | flops 25165824 | bytes 12608512 | tf_op jit(solution)/shard_map/dot_general | solution.py:33
  89.5 0.4 fusion.22
  90.0 82.0 %all-reduce.1 = (f32[512]{0:T(512)S(1)}, f32[6144]{0:T(1024)S(1)}) all-reduce(f32[512]{0:T(512)S(1)} %bitcast.42, f32[6144]{0:T(1024)S(1)} %bitcast.39), channel_id=1, replica_groups=mesh['band'=16,'ga'=2] {'band'}, use_global_device_ids=true, to_apply=%region_3.4 | all-reduce | flops 6656 | bytes 53248 | tf_op jit(solution)/shard_map/psum | solution.py:57
  172.0 0.1 dynamic-slice_multiply_fusion
  172.0 267.9 %reduce-scatter.2.cloned.1.call-done = f32[384,1024]{1,0:T(8,128)} async-done(((f32[6144,1024]{1,0:T(8,128)}), f32[384,1024]{1,0:T(8,128)}) %reduce-scatter.2.cloned.1.call-update) | async-done | bytes 1572880 | tf_op jit(solution)/shard_map/reduce_scatter | solution.py:53
  439.9 1.6 broadcast_multiply_fusion
  441.5 0.4 fusion.21
  441.9 0.1 pad_maximum_fusion
  442.1 2.4 copy.7
  (7 shorter events, 0.0 us)
Async XLA Ops:
  6.5 25.3 %all-reduce.4.cloned.1.call-start = ((), (), s32[]{:S(2)}) async-start(), calls=%async_computation.1 | async-start | bytes 2097152 | tf_op jit(solution)/shard_map/psum | solution.py:12
  8.8 431.1 %reduce-scatter.2.cloned.1.call-start = ((), (), s32[]{:S(2)}) async-start(), calls=%async_computation.2 | async-start | bytes 26738688 | tf_op jit(solution)/shard_map/reduce_scatter | solution.py:53
  79.0 0.8 copy-start.1
  79.0 0.9 copy-start.2
  79.0 10.6 %copy-start = (f32[2,256,512]{2,1,0:T(8,128)S(1)}, f32[2,256,512]{2,1,0:T(8,128)}, u32[]{:S(2)}) copy-start(f32[2,256,512]{2,1,0:T(8,128)} %all-reduce.4.cloned.1.call-done) | copy-start | bytes 3145732
  81.1 360.4 %slice-start = ((f32[12288]{0:T(1024)}), f32[512]{0:T(512)S(1)}, s32[]{:S(2)}) async-start(f32[12288]{0:T(1024)} %param.9), calls=%async_computation.3 | async-start | bytes 4096 | tf_op jit(solution)/shard_map/slice | solution.py:62
Sparse Core Ops, SparseCore 0:
  9.7 22.1 all-reduce.3
  79.1 360.7 reduce-scatter.1
where the time goes:
time: 452 us; the launch traced here: 451 us
  waiting for transfers between devices  278 us (62%)
  blocking collectives  82 us (18%)
  matrix products  53.6 us (12%)
  other arithmetic  17.7 us (4%)
  between operations  14.8 us (3%)
  local copies, waits for them, and re-layouts  5.05 us (1%)
    reduce_scatter x1, waiting for transfers between devices, body(): lax.psum_scatter(contract(left, right), 'band', scatter_dimension=0, tile...  268 us
    psum x1, blocking collectives, body(): col_def = lax.psum(defect_slab, 'band')  82 us
    dot_general x1, matrix products, contract(): lax.dot_general(left, right, (((0,), (0,)), ((), ())), precision=lax.Prec...  44.8 us
    mul x1, other arithmetic, body(): coef[:, None] * matrix_elements[0]  11.4 us
    psum x1, waiting for transfers between devices, spread(): return lax.psum(jnp.where(mine, x, jnp.zeros_like(x)), axis)  10.2 us
  transfers between devices with their start and end apart: 2, of which 2 were waited for; matrix products, arithmetic and copies ran while one was open for 5% of the time, Pallas kernels for 0%

commit v1 on v0

--- a/solution.py
+++ b/solution.py
@@ -5,6 +5,7 @@
 from jax.sharding import PartitionSpec as P
 
 COLS = 512
+plan_squares = lambda shard_axis, frame: jnp.sum(lax.all_gather(frame, axis_name=shard_axis), 0)
 
 
 def spread(x, axis, root):
@@ -54,7 +55,7 @@
     defect_full = defects(coef, matrix_elements)
     defect_slab = defects(coef, slab)
     row_def = lax.psum_scatter(defect_full, "band", scatter_dimension=0, tiled=True)
-    col_def = lax.psum(defect_slab, "band")
+    col_def = plan_squares("band", defect_slab)
     sums = sums * factor
     row_def = row_def * factor
     col_def = col_def * factor

time: 452 us -> 453 us (level)
  blocking collectives: 82 us -> 119 us
  waiting for transfers between devices: 278 us -> 242 us
    psum x1 -> x0, blocking collectives: 82 us -> none  [body(): col_def = lax.psum(defect_slab, 'band')]
    unnamed x0 -> x1, blocking collectives: none -> 81.8 us
    all_gather x0 -> x1, blocking collectives: none -> 37.6 us  [lax.all_gather(frame, axis_name=shard_axis)]
    reduce_scatter x1, waiting for transfers between devices: 268 us -> 232 us  [body(): lax.psum_scatter(contract(left, right), 'band', scatter_dimension=0, tile...]
where the time goes in v1:
time: 453 us; the launch traced here: 452 us
  waiting for transfers between devices  242 us (53%)
  blocking collectives  119 us (26%)
  matrix products  53.6 us (12%)
  other arithmetic  17.7 us (4%)
  between operations  14.8 us (3%)
  local copies, waits for them, and re-layouts  5.05 us (1%)
    reduce_scatter x1, waiting for transfers between devices, body(): lax.psum_scatter(contract(left, right), 'band', scatter_dimension=0, tile...  232 us
    unnamed x1, blocking collectives  81.8 us
    dot_general x1, matrix products, contract(): lax.dot_general(left, right, (((0,), (0,)), ((), ())), precision=lax.Prec...  44.8 us
    all_gather x1, blocking collectives, lax.all_gather(frame, axis_name=shard_axis)  37.6 us
    mul x1, other arithmetic, body(): coef[:, None] * matrix_elements[0]  11.4 us
    psum x1, waiting for transfers between devices, spread(): return lax.psum(jnp.where(mine, x, jnp.zeros_like(x)), axis)  10.2 us
  transfers between devices with their start and end apart: 2, of which 2 were waited for; matrix products, arithmetic and copies ran while one was open for 5% of the time, Pallas kernels for 0%

profile of v1, /device:TPU:0, one launch (start us, length us, event | category | flops | bytes accessed | tf_op | source)
XLA Modules:
  0.0 452.4 jit_solution(7595040104415083493)
XLA Ops:
  6.5 2.3 slice_select_fusion
  8.8 0.0 all-reduce.3.cloned.1.call-update
  8.8 0.0 reduce-scatter.2.cloned.1.call-start
  9.5 0.7 fusion.28
  10.2 11.4 %bitcast_multiply_fusion.3 = (f32[256,6144]{1,0:T(8,128)}, f32[256,6144]{1,0:T(8,128)}) fusion(f32[2,256,6144]{2,1,0:T(8,128)} %param.5, f32[256]{0:T(256)S(1)} %fusion.28), kind=kLoop, calls=%fused_computation.9 | loop fusion | flops 3145728 | bytes 25166848 | tf_op jit(solution)/shard_map/mul | solution.py:51
  21.7 10.2 %all-reduce.3.cloned.1.call-done = f32[2,256,512]{2,1,0:T(8,128)} async-done(((f32[2,256,512]{2,1,0:T(8,128)}), f32[2,256,512]{2,1,0:T(8,128)}) %all-reduce.3.cloned.1.call-update) | async-done | bytes 1048592 | tf_op jit(solution)/shard_map/psum | solution.py:13
  31.8 1.1 fusion.32
  32.9 1.3 slice_bitcast_fusion.1
  34.2 44.8 %fusion = f32[6144,1024]{1,0:T(8,128)} fusion(f32[256,6144]{1,0:T(8,128)} %get-tuple-element.6, f32[256,6144]{1,0:T(8,128)} %get-tuple-element.5, f32[256,512]{1,0:T(8,128)S(1)} %fusion.32, f32[256,512]{1,0:T(8,128)S(1)} %get-tuple-element.10, f32[256,512]{1,0:T(8,128)S(1)} %get-tuple-element.9), kind=kOutput, calls=%fused_computation | convolution fusion | flops 38659424256 | bytes 39321600 | tf_op jit(solution)/shard_map/dot_general | solution.py:17
  79.0 0.0 reduce-scatter.2.cloned.1.call-update
  79.0 0.7 copy-done.1
  79.8 0.1 dynamic_slice.3
  79.8 0.6 dynamic-slice
  81.1 0.0 slice-start
  81.1 8.5 %fusion.5 = f32[1,6144]{1,0:T(1,128)S(1)} fusion(f32[256,1]{0,1:T(1,128)S(1)} %bitcast.43, f32[2,256,6144]{2,1,0:T(8,128)} %param.5), kind=kOutput, calls=%fused_computation.7 | convolution fusion | flops 25165824 | bytes 12608512 | tf_op jit(solution)/shard_map/dot_general | solution.py:34
  89.5 81.8 %all-reduce = f32[6144]{0:T(1024)S(1)} all-reduce(f32[6144]{0:T(1024)S(1)} %bitcast.42), channel_id=4, replica_groups=mesh['band'=16,'ga'=2] {'band'}, use_global_device_ids=true, to_apply=%region_2.3.clone | all-reduce | flops 6144 | bytes 49152
  171.3 0.1 dynamic-slice_multiply_fusion
  171.4 0.4 convolution_bitcast_fusion
  171.8 37.6 %all-gather.1 = f32[16,1,512]{2,1,0:T(1,128)S(1)} all-gather(f32[1,1,512]{2,1,0:T(1,128)S(1)} %convolution_bitcast_fusion), channel_id=2, replica_groups=mesh['band'=16,'ga'=2] {'band'}, dimensions={0}, use_global_device_ids=true | all-gather | bytes 34816 | tf_op jit(solution)/shard_map/all_gather | solution.py:8
  209.5 231.6 %reduce-scatter.2.cloned.1.call-done = f32[384,1024]{1,0:T(8,128)} async-done(((f32[6144,1024]{1,0:T(8,128)}), f32[384,1024]{1,0:T(8,128)}) %reduce-scatter.2.cloned.1.call-update) | async-done | bytes 1572880 | tf_op jit(solution)/shard_map/reduce_scatter | solution.py:54
  441.1 1.6 broadcast_multiply_fusion
  442.7 0.4 fusion.21
  443.1 0.1 pad_maximum_fusion
  443.2 2.4 copy.7
  (9 shorter events, 0.1 us)
Async XLA Ops:
  6.5 25.3 %all-reduce.3.cloned.1.call-start = ((), (), s32[]{:S(2)}) async-start(), calls=%async_computation.1 | async-start | bytes 2097152 | tf_op jit(solution)/shard_map/psum | solution.py:13
  8.8 432.2 %reduce-scatter.2.cloned.1.call-start = ((), (), s32[]{:S(2)}) async-start(), calls=%async_computation.2 | async-start | bytes 26738688 | tf_op jit(solution)/shard_map/reduce_scatter | solution.py:54
  79.0 0.8 copy-start.1
  79.0 0.9 copy-start.2
  79.0 92.4 %copy-start = (f32[2,256,512]{2,1,0:T(8,128)S(1)}, f32[2,256,512]{2,1,0:T(8,128)}, u32[]{:S(2)}) copy-start(f32[2,256,512]{2,1,0:T(8,128)} %all-reduce.3.cloned.1.call-done) | copy-start | bytes 3145732
  81.1 361.6 %slice-start = ((f32[12288]{0:T(1024)}), f32[512]{0:T(512)S(1)}, s32[]{:S(2)}) async-start(f32[12288]{0:T(1024)} %param.9), calls=%async_computation.3 | async-start | bytes 4096 | tf_op jit(solution)/shard_map/slice | solution.py:63
Sparse Core Ops, SparseCore 0:
  9.7 22.1 all-reduce.2
  79.1 361.9 reduce-scatter.1
